TPU v7x, 32 devices: a whole 2x2x4 slice. The times are simulated.
32 devices in a mesh: rows: 8 (over y, x, core), sub: 4 (over z).
Axes of the slice: x: 2, y: 2, z: 4, core: 2. Of those that a mesh axis runs over, the one named last changes fastest.
Arguments:
- u_fem: float32 [120, 524288], P(None, ('rows', 'sub')), may hold values from -600 to 600
- resid_fem: float32 [1, 524288], P(None, ('rows', 'sub')), may hold values from -60 to 60
- slot_map: int32 [32, 32], P(('rows', 'sub')), may hold values from 0 to 31, as said below
- restart: float32 [120, 40], replicated, may hold values from -0.5 to 0.5
- coeff: float32 [3, 120, 120], P(None, None, 'sub'), may hold values from -6 to 6
Outputs:
- new_basis: float32 [40, 524288], P(None, ('rows', 'sub'))
- next_vector: float32 [1, 524288], P(None, ('rows', 'sub'))
- new_coeff: float32 [3, 40, 120], replicated
Inputs may be any that keep to these rules, and one draw needn't show every extreme that they name: Each row of slot_map is a permutation of 0 to 31.
All inputs are finite; a program needn't handle non-finite values.
Results may differ from a plain program's by a relative error of at most 0.00015.
Values sent between devices are 32-bit elements; how exact they have to be, the bound alone decides.
A program may use at most 64 MiB of HBM per device.

v0:
```python
import jax
import jax.numpy as jnp
from jax import lax
from jax.sharding import PartitionSpec as P


def settle(values, source, dev_count):
    width = values.shape[0]
    block_len = values.shape[1] // dev_count
    blocks = values.reshape(width, dev_count, block_len)
    return jnp.take(blocks, source, axis=1).reshape(width, dev_count * block_len)


def local(u_fem, resid_fem, slot_map, restart, coeff):
    highest = lax.Precision.HIGHEST
    dev_count = lax.axis_size(("rows", "sub"))
    nrows_all = u_fem.shape[1] * dev_count
    source = jnp.argsort(slot_map[0])
    basis_rows, resid_row = (u_fem, resid_fem)
    gram_local = jnp.einsum("kn,jn->kj", basis_rows, basis_rows, precision=highest)
    inner_local = jnp.einsum("kn,n->k", basis_rows, resid_row[0], precision=highest)
    gram_sum = lax.psum(gram_local, ("rows", "sub"))
    chol_lower = jnp.linalg.cholesky(gram_sum / nrows_all)
    factor = lax.linalg.triangular_solve(
        chol_lower, restart, left_side=True, lower=True, transpose_a=True
    )
    new_rows = jnp.einsum("kp,kn->pn", factor, basis_rows, precision=highest)
    inner_prod = lax.psum(inner_local, ("rows", "sub"))
    half_solve = lax.linalg.triangular_solve(
        chol_lower, inner_prod[:, None], left_side=True, lower=True
    )
    proj_coef = (
        lax.linalg.triangular_solve(
            chol_lower, half_solve, left_side=True, lower=True, transpose_a=True
        )[:, 0]
        / nrows_all
    )
    remainder = resid_row - jnp.einsum("k,kn->n", proj_coef, basis_rows, precision=highest)[None, :]
    norm_sum = lax.psum(jnp.sum(remainder * remainder), ("rows", "sub"))
    next_row = remainder * lax.rsqrt(norm_sum / nrows_all + 1e-06)
    new_rows, next_row = (
        lax.all_to_all(new_rows, ("rows", "sub"), split_axis=1, concat_axis=1, tiled=True),
        lax.all_to_all(next_row, ("rows", "sub"), split_axis=1, concat_axis=1, tiled=True),
    )
    new_rows = settle(new_rows, source, dev_count)
    next_row = settle(next_row, source, dev_count)
    raised = jnp.dot(chol_lower, restart, precision=highest)
    coeff_all = lax.all_gather(coeff, "sub", axis=2, tiled=True)
    rotated = jnp.einsum("kp,ikm->ipm", raised, coeff_all, precision=highest)
    new_coeff = rotated * lax.rsqrt(jnp.mean(rotated * rotated) + 1e-06)
    return (new_rows, next_row, new_coeff)


def solution(mesh):
    in_specs = (
        P(None, ("rows", "sub")),
        P(None, ("rows", "sub")),
        P(("rows", "sub"), None),
        P(),
        P(None, None, "sub"),
    )
    out_specs = (P(None, ("rows", "sub")), P(None, ("rows", "sub")), P())
    return jax.shard_map(local, mesh=mesh, in_specs=in_specs, out_specs=out_specs, check_vma=False)
```

profile of v0, /device:TPU:0, one launch (start us, length us, event | category | flops | bytes accessed | tf_op | source)
XLA Modules:
  0.0 229.9 jit_solution(9403381852364649270)
XLA Ops:
  0.6 0.0 copy-start
  0.6 0.0 copy-start.1
  0.7 0.0 copy-start.2
  0.7 10.1 %fusion.16 = f32[120,120]{0,1:T(8,128)S(1)} fusion(f32[120,16384]{1,0:T(8,128)} %param.5), kind=kOutput, calls=%fused_computation.44 | convolution fusion | flops 2831155200 | bytes 7921920 | tf_op jit(solution)/shard_map/kn,jn->kj/dot_general | solution.py:20
  10.7 0.0 copy-done.1
  10.7 0.0 copy-done.2
  10.8 6.2 %convolution_bitcast_fusion.3 = f32[120]{0:T(128)S(1)} fusion(f32[120,16384]{1,0:T(8,128)S(1)} %copy-done.1, f32[1,16384]{1,0:T(1,128)S(1)} %copy-done.2), kind=kOutput, calls=%fused_computation.10 | convolution fusion | flops 23592960 | bytes 7930336 | tf_op jit(solution)/shard_map/kn,n->k/dot_general | solution.py:21
  16.9 42.8 %all-reduce = (f32[120,120]{0,1:T(8,128)S(1)}, f32[120]{0:T(128)S(1)}) all-reduce(f32[120,120]{0,1:T(8,128)S(1)} %fusion.16, f32[120]{0:T(128)S(1)} %convolution_bitcast_fusion.3), channel_id=1, replica_groups=mesh['rows'=8,'sub'=4] {'rows','sub'}, use_global_device_ids=true, to_apply=%region_1.2 | all-reduce | flops 14520 | bytes 116160 | tf_op jit(solution)/shard_map/psum | solution.py:22
  59.8 0.1 copy.18
  59.9 11.0 %cholesky.16 = f32[120,120]{1,0:T(8,128)S(1)} custom-call(f32[120,120]{1,0:T(8,128)S(1)} %fusion.9), custom_call_target="Cholesky" | custom-call | tf_op jit(solution)/shard_map/jit(cholesky)/cholesky | solution.py:23
  70.9 0.6 compare_reduce_fusion
  71.5 0.7 select_bitcast_fusion
  72.2 9.2 %custom-call.10 = f32[1,120,120]{1,2,0:T(8,128)S(1)} custom-call(f32[1,120,120]{2,1,0:T(8,128)S(1)} %select_bitcast_fusion), custom_call_target="InvertDiagBlocksLowerTriangular" | custom-call | tf_op jit(solution)/shard_map/triangular_solve | solution.py:24
  81.4 0.2 convolution_bitcast_fusion.2
  81.6 0.2 fusion.1
  81.8 6.7 %multiply_reduce_fusion = (f32[]{:T(128)}, f32[1,16384]{1,0:T(1,128)S(1)}) fusion(f32[1,16384]{1,0:T(1,128)S(1)} %copy-done.2, f32[120,1]{0,1:T(1,128)S(1)} %fusion.1, f32[120,16384]{1,0:T(8,128)} %param.5), kind=kOutput, calls=%fused_computation.15 | convolution fusion | flops 23642112 | bytes 7995876 | tf_op jit(solution)/shard_map/k,kn->n/dot_general | solution.py:38
  88.5 40.3 %psum.23 = f32[]{:T(128)} all-reduce(f32[]{:T(128)} %get-tuple-element.7), channel_id=1, replica_groups=mesh['rows'=8,'sub'=4] {'rows','sub'}, use_global_device_ids=true, to_apply=%region_6.7 | all-reduce | flops 1 | bytes 8 | tf_op jit(solution)/shard_map/psum | solution.py:39
  129.5 0.7 broadcast_multiply_fusion
  130.1 5.4 %all-to-all-start.1 = ((f32[1,32,512]{2,0,1:T(1,128)}), f32[1,32,512]{2,0,1:T(1,128)S(1)}, u32[]{:S(2)}, u32[]{:S(2)}) async-start(f32[1,32,512]{2,0,1:T(1,128)} %bitcast.14), calls=%async_computation.1 | async-start | bytes 131072 | tf_op jit(solution)/shard_map/all_to_all | solution.py:43
  135.5 0.0 copy-done
  135.6 0.2 fusion.7
  135.8 0.0 copy-start.4
  135.8 6.5 %fusion.17 = f32[40,16384]{1,0:T(8,128)S(1)} fusion(f32[120,40]{0,1:T(8,128)S(1)} %fusion.7, f32[120,16384]{1,0:T(8,128)} %param.5), kind=kOutput, calls=%fused_computation.45 | convolution fusion | flops 943718400 | bytes 10504960 | tf_op jit(solution)/shard_map/kp,kn->pn/dot_general | solution.py:27
  142.3 0.0 copy-start.3
  142.3 1.7 copy.36
  144.1 0.0 copy-done.4
  144.1 1.7 sort.17
  145.8 0.0 all-to-all-done.1
  145.8 5.8 %all-to-all-start = ((f32[40,32,512]{2,0,1:T(8,128)}), f32[40,32,512]{2,0,1:T(8,128)S(1)}, u32[]{:S(2)}, u32[]{:S(2)}) async-start(f32[40,32,512]{2,0,1:T(8,128)} %bitcast.69), calls=%async_computation | async-start | bytes 5242880 | tf_op jit(solution)/shard_map/all_to_all | solution.py:42
  151.6 0.1 broadcast_bitcast_fusion
  151.7 0.1 copy.28
  151.8 0.0 copy-done.3
  151.8 67.3 %all_gather.3 = f32[3,120,120]{1,0,2:T(4,128)S(1)} all-gather(f32[3,120,30]{1,0,2:T(4,128)S(1)} %copy.21), channel_id=1, replica_groups=mesh['rows'=8,'sub'=4] {'sub'}, dimensions={2}, use_global_device_ids=true | all-gather | bytes 216000 | tf_op jit(solution)/shard_map/all_gather | solution.py:48
  219.1 0.9 convolution_bitcast_fusion
  220.0 1.0 multiply_reduce_fusion.1
  221.8 0.1 broadcast_bitcast_fusion.1
  221.9 0.6 multiply_bitcast_fusion
  222.5 0.6 gather_fusion.1
  223.1 0.1 copy.29
  223.2 0.7 broadcast_select_fusion.1
  223.9 0.0 all-to-all-done
  223.9 2.2 gather_fusion
  226.2 2.1 copy.26
  228.2 1.7 broadcast_select_fusion
  (10 shorter events, 0.1 us)
Async XLA Ops:
  0.6 134.9 %copy-start = (f32[120,40]{0,1:T(8,128)S(1)}, f32[120,40]{0,1:T(8,128)}, u32[]{:S(2)}) copy-start(f32[120,40]{0,1:T(8,128)} %param.8) | copy-start | bytes 57604
  0.6 10.1 %copy-start.1 = (f32[120,16384]{1,0:T(8,128)S(1)}, f32[120,16384]{1,0:T(8,128)}, u32[]{:S(2)}) copy-start(f32[120,16384]{1,0:T(8,128)} %param.5) | copy-start | bytes 23592964
  0.7 10.1 %copy-start.2 = (f32[1,16384]{1,0:T(1,128)S(1)}, f32[1,16384]{1,0:T(1,128)}, u32[]{:S(2)}) copy-start(f32[1,16384]{1,0:T(1,128)} %param.6) | copy-start | bytes 196612
  130.1 15.6 %all-to-all-start.1 = ((f32[1,32,512]{2,0,1:T(1,128)}), f32[1,32,512]{2,0,1:T(1,128)S(1)}, u32[]{:S(2)}, u32[]{:S(2)}) async-start(f32[1,32,512]{2,0,1:T(1,128)} %bitcast.14), calls=%async_computation.1 | async-start | bytes 131072 | tf_op jit(solution)/shard_map/all_to_all | solution.py:43
  135.8 8.3 %copy-start.4 = (s32[1,32]{1,0:T(1,128)S(1)}, s32[1,32]{1,0:T(1,128)}, u32[]{:S(2)}) copy-start(s32[1,32]{1,0:T(1,128)} %param.7) | copy-start | bytes 388
  142.3 9.4 %copy-start.3 = (f32[3,120,30]{1,2,0:T(8,128)S(1)}, f32[3,120,30]{1,2,0:T(8,128)}, u32[]{:S(2)}) copy-start(f32[3,120,30]{1,2,0:T(8,128)} %param.9) | copy-start | bytes 129604
  145.8 78.2 %all-to-all-start = ((f32[40,32,512]{2,0,1:T(8,128)}), f32[40,32,512]{2,0,1:T(8,128)S(1)}, u32[]{:S(2)}, u32[]{:S(2)}) async-start(f32[40,32,512]{2,0,1:T(8,128)} %bitcast.69), calls=%async_computation | async-start | bytes 5242880 | tf_op jit(solution)/shard_map/all_to_all | solution.py:42
where the time goes:
time: 231 us; the launch traced here: 230 us
  blocking collectives  150 us (65%)
  matrix products  32 us (14%)
  other arithmetic  27 us (12%)
  starting transfers between devices  11.2 us (5%)
  local copies, waits for them, and re-layouts  7.06 us (3%)
    all_gather x1, blocking collectives, local(): coeff_all = lax.all_gather(coeff, 'sub', axis=2, tiled=True)  67.3 us
    psum x1, blocking collectives, local(): gram_sum = lax.psum(gram_local, ('rows', 'sub'))  42.8 us
    psum x1, blocking collectives, local(): norm_sum = lax.psum(jnp.sum(remainder * remainder), ('rows', 'sub'))  40.3 us
    another operation x3, other arithmetic, local(): chol_lower = jnp.linalg.cholesky(gram_sum / nrows_all)  11.6 us
    dot_general x1, matrix products, local(): jnp.einsum('kn,jn->kj', basis_rows, basis_rows, precision=highest)  10.1 us
    another operation x2, other arithmetic, local(): lax.linalg.triangular_solve(chol_lower, restart, left_side=True, lower=Tr...  9.85 us
    dot_general x1, matrix products, local(): jnp.einsum('k,kn->n', proj_coef, basis_rows, precision=highest)[None, :]  6.74 us
    dot_general x1, matrix products, local(): new_rows = jnp.einsum('kp,kn->pn', factor, basis_rows, precision=highest)  6.51 us
  transfers between devices with their start and end apart: 2, of which 0 were waited for; matrix products, arithmetic and copies ran while one was open for 6% of the time, Pallas kernels for 0%

commit v1 on v0

--- a/solution.py
+++ b/solution.py
@@ -19,7 +19,7 @@
     basis_rows, resid_row = (u_fem, resid_fem)
     gram_local = jnp.einsum("kn,jn->kj", basis_rows, basis_rows, precision=highest)
     inner_local = jnp.einsum("kn,n->k", basis_rows, resid_row[0], precision=highest)
-    gram_sum = lax.psum(gram_local, ("rows", "sub"))
+    gram_sum = jnp.sum(lax.all_gather(gram_local, ("rows", "sub")), axis=0)
     chol_lower = jnp.linalg.cholesky(gram_sum / nrows_all)
     factor = lax.linalg.triangular_solve(
         chol_lower, restart, left_side=True, lower=True, transpose_a=True

time: 231 us -> 253 us (1.095)
  between operations: 2.26 us -> 15.6 us
  waiting for transfers between devices: 0.01 us -> 6.92 us
  matrix products: 32 us -> 34.7 us
    all_gather x0 -> x1, waiting for transfers between devices: none -> 6.9 us  [local(): gram_sum = jnp.sum(lax.all_gather(gram_local, ('rows', 'sub')), axis=0)]
  transfers between devices with their start and end apart: 2 -> 3, of which waited for: 0 -> 1; matrix products, arithmetic and copies ran while one was open for 6% -> 9% of each run, Pallas kernels for 0% -> 0%
where the time goes in v1:
time: 253 us; the launch traced here: 252 us
  blocking collectives  148 us (58%)
  matrix products  34.7 us (14%)
  other arithmetic  28.6 us (11%)
  between operations  15.6 us (6%)
  starting transfers between devices  11.3 us (4%)
  local copies, waits for them, and re-layouts  6.97 us (3%)
  waiting for transfers between devices  6.92 us (3%)
    all_gather x1, blocking collectives, local(): coeff_all = lax.all_gather(coeff, 'sub', axis=2, tiled=True)  67.2 us
    psum x1, blocking collectives, local(): inner_prod = lax.psum(inner_local, ('rows', 'sub'))  42.1 us
    psum x1, blocking collectives, local(): norm_sum = lax.psum(jnp.sum(remainder * remainder), ('rows', 'sub'))  38.6 us
    another operation x3, other arithmetic, local(): chol_lower = jnp.linalg.cholesky(gram_sum / nrows_all)  11.6 us
    dot_general x1, matrix products, local(): jnp.einsum('kn,jn->kj', basis_rows, basis_rows, precision=highest)  10.5 us
    another operation x2, other arithmetic, local(): lax.linalg.triangular_solve(chol_lower, restart, left_side=True, lower=Tr...  9.85 us
    dot_general x1, matrix products, local(): jnp.einsum('kn,n->k', basis_rows, resid_row[0], precision=highest)  8.41 us
    all_gather x1, waiting for transfers between devices, local(): gram_sum = jnp.sum(lax.all_gather(gram_local, ('rows', 'sub')), axis=0)  6.9 us
  transfers between devices with their start and end apart: 3, of which 1 were waited for; matrix products, arithmetic and copies ran while one was open for 9% of the time, Pallas kernels for 0%

profile of v1, /device:TPU:0, one launch (start us, length us, event | category | flops | bytes accessed | tf_op | source)
XLA Modules:
  0.0 252.0 jit_solution(6336451378936123688)
XLA Ops:
  7.2 0.0 copy-start
  7.2 0.0 copy-start.3
  7.2 0.0 copy-start.1
  7.2 0.0 all-gather.3.cloned.1.call-start
  7.2 10.5 %fusion.16 = f32[120,120]{1,0:T(8,128)} fusion(f32[120,16384]{1,0:T(8,128)} %param.5), kind=kOutput, calls=%fused_computation.43 | convolution fusion | flops 2831155200 | bytes 7921920 | tf_op jit(solution)/shard_map/kn,jn->kj/dot_general | solution.py:20
  17.8 0.0 all-gather.3.cloned.1.call-update
  17.8 0.0 copy-done.3
  17.8 1.6 sort.17
  19.4 0.0 copy-done.1
  19.4 8.4 %convolution_bitcast_fusion.3 = f32[120]{0:T(128)S(1)} fusion(f32[120,16384]{1,0:T(8,128)} %param.5, f32[1,16384]{1,0:T(1,128)S(1)} %copy-done.1), kind=kOutput, calls=%fused_computation.10 | convolution fusion | flops 23592960 | bytes 7930336 | tf_op jit(solution)/shard_map/kn,n->k/dot_general | solution.py:21
  27.8 42.1 %psum.14 = f32[120]{0:T(128)S(1)} all-reduce(f32[120]{0:T(128)S(1)} %convolution_bitcast_fusion.3), channel_id=1, replica_groups=mesh['rows'=8,'sub'=4] {'rows','sub'}, use_global_device_ids=true, to_apply=%region_4.5 | all-reduce | flops 120 | bytes 960 | tf_op jit(solution)/shard_map/psum | solution.py:28
  70.0 6.9 %all-gather.3.cloned.1.call-done = f32[3840,120]{1,0:T(8,128)} async-done(((f32[120,120]{1,0:T(8,128)}), f32[3840,120]{1,0:T(8,128)}) %all-gather.3.cloned.1.call-update) | async-done | bytes 1843216 | tf_op jit(solution)/shard_map/all_gather | solution.py:22
  76.9 1.7 reduce_sum.29
  78.6 0.1 copy.14
  78.7 11.0 %cholesky.16 = f32[120,120]{1,0:T(8,128)S(1)} custom-call(f32[120,120]{1,0:T(8,128)S(1)} %fusion.9), custom_call_target="Cholesky" | custom-call | tf_op jit(solution)/shard_map/jit(cholesky)/cholesky | solution.py:23
  89.7 0.6 compare_reduce_fusion
  90.3 0.7 select_bitcast_fusion
  91.0 9.2 %custom-call.10 = f32[1,120,120]{1,2,0:T(8,128)S(1)} custom-call(f32[1,120,120]{2,1,0:T(8,128)S(1)} %select_bitcast_fusion), custom_call_target="InvertDiagBlocksLowerTriangular" | custom-call | tf_op jit(solution)/shard_map/triangular_solve | solution.py:24
  100.2 0.2 convolution_bitcast_fusion.2
  100.4 0.2 fusion.1
  100.6 6.7 %multiply_reduce_fusion = (f32[]{:T(128)}, f32[1,16384]{1,0:T(1,128)S(1)}) fusion(f32[1,16384]{1,0:T(1,128)S(1)} %copy-done.1, f32[120,1]{0,1:T(1,128)S(1)} %fusion.1, f32[120,16384]{1,0:T(8,128)} %param.5), kind=kOutput, calls=%fused_computation.15 | convolution fusion | flops 23642112 | bytes 7995876 | tf_op jit(solution)/shard_map/k,kn->n/dot_general | solution.py:38
  107.3 38.6 %psum.15 = f32[]{:T(128)} all-reduce(f32[]{:T(128)} %get-tuple-element.5), channel_id=1, replica_groups=mesh['rows'=8,'sub'=4] {'rows','sub'}, use_global_device_ids=true, to_apply=%region_6.7 | all-reduce | flops 1 | bytes 8 | tf_op jit(solution)/shard_map/psum | solution.py:39
  146.5 0.7 broadcast_multiply_fusion
  147.2 5.5 %all-to-all-start.1 = ((f32[1,32,512]{2,0,1:T(1,128)}), f32[1,32,512]{2,0,1:T(1,128)S(1)}, u32[]{:S(2)}, u32[]{:S(2)}) async-start(f32[1,32,512]{2,0,1:T(1,128)} %bitcast.15), calls=%async_computation.1 | async-start | bytes 131072 | tf_op jit(solution)/shard_map/all_to_all | solution.py:43
  152.7 0.0 copy-done
  152.7 0.2 fusion.7
  153.0 6.5 %fusion.17 = f32[40,16384]{1,0:T(8,128)S(1)} fusion(f32[120,40]{0,1:T(8,128)S(1)} %fusion.7, f32[120,16384]{1,0:T(8,128)} %param.5), kind=kOutput, calls=%fused_computation.44 | convolution fusion | flops 943718400 | bytes 10504960 | tf_op jit(solution)/shard_map/kp,kn->pn/dot_general | solution.py:27
  159.5 0.0 copy-start.2
  159.5 1.7 copy.31
  161.2 0.0 all-to-all-done.1
  161.2 5.8 %all-to-all-start = ((f32[40,32,512]{2,0,1:T(8,128)}), f32[40,32,512]{2,0,1:T(8,128)S(1)}, u32[]{:S(2)}, u32[]{:S(2)}) async-start(f32[40,32,512]{2,0,1:T(8,128)} %bitcast.70), calls=%async_computation | async-start | bytes 5242880 | tf_op jit(solution)/shard_map/all_to_all | solution.py:42
  167.1 0.1 broadcast_bitcast_fusion
  167.1 0.1 copy.23
  167.2 0.0 copy-done.2
  167.3 0.1 broadcast_bitcast_fusion.1
  167.4 67.2 %all_gather.11 = f32[3,120,120]{1,0,2:T(4,128)S(1)} all-gather(f32[3,120,30]{1,0,2:T(4,128)S(1)} %copy.17), channel_id=1, replica_groups=mesh['rows'=8,'sub'=4] {'sub'}, dimensions={2}, use_global_device_ids=true | all-gather | bytes 216000 | tf_op jit(solution)/shard_map/all_gather | solution.py:48
  234.6 0.9 convolution_bitcast_fusion
  235.5 1.0 multiply_reduce_fusion.1
  237.2 0.6 multiply_bitcast_fusion
  237.9 0.6 gather_fusion.1
  238.5 0.1 copy.24
  238.5 0.7 broadcast_select_fusion.1
  239.3 0.0 all-to-all-done
  239.3 2.2 gather_fusion
  241.5 2.0 copy.21
  243.5 1.7 broadcast_select_fusion
  (9 shorter events, 0.1 us)
Async XLA Ops:
  7.2 145.5 %copy-start = (f32[120,40]{0,1:T(8,128)S(1)}, f32[120,40]{0,1:T(8,128)}, u32[]{:S(2)}) copy-start(f32[120,40]{0,1:T(8,128)} %param.8) | copy-start | bytes 57604
  7.2 10.6 %copy-start.3 = (s32[1,32]{1,0:T(1,128)S(1)}, s32[1,32]{1,0:T(1,128)}, u32[]{:S(2)}) copy-start(s32[1,32]{1,0:T(1,128)} %param.7) | copy-start | bytes 388
  7.2 12.2 %copy-start.1 = (f32[1,16384]{1,0:T(1,128)S(1)}, f32[1,16384]{1,0:T(1,128)}, u32[]{:S(2)}) copy-start(f32[1,16384]{1,0:T(1,128)} %param.6) | copy-start | bytes 196612
  7.2 69.7 %all-gather.3.cloned.1.call-start = ((), (), s32[]{:S(2)}) async-start(), calls=%async_computation.2 | async-start | bytes 2027520 | tf_op jit(solution)/shard_map/all_gather | solution.py:22
  147.2 14.0 %all-to-all-start.1 = ((f32[1,32,512]{2,0,1:T(1,128)}), f32[1,32,512]{2,0,1:T(1,128)S(1)}, u32[]{:S(2)}, u32[]{:S(2)}) async-start(f32[1,32,512]{2,0,1:T(1,128)} %bitcast.15), calls=%async_computation.1 | async-start | bytes 131072 | tf_op jit(solution)/shard_map/all_to_all | solution.py:43
  159.5 7.7 %copy-start.2 = (f32[3,120,30]{1,2,0:T(8,128)S(1)}, f32[3,120,30]{1,2,0:T(8,128)}, u32[]{:S(2)}) copy-start(f32[3,120,30]{1,2,0:T(8,128)} %param.9) | copy-start | bytes 129604
  161.2 78.1 %all-to-all-start = ((f32[40,32,512]{2,0,1:T(8,128)}), f32[40,32,512]{2,0,1:T(8,128)S(1)}, u32[]{:S(2)}, u32[]{:S(2)}) async-start(f32[40,32,512]{2,0,1:T(8,128)} %bitcast.70), calls=%async_computation | async-start | bytes 5242880 | tf_op jit(solution)/shard_map/all_to_all | solution.py:42
Sparse Core Ops, SparseCore 0:
  17.9 58.9 all-gather.2
